TPU v7x, 512 devices: a whole 4x8x8 slice. The times are simulated.
512 devices in a mesh: gx: 8 (over z_lo, core), gy: 8 (over y), gz: 8 (over x, z_hi).
Axes of the slice: x: 4, y: 8, z: 8 (z_hi: 2, z_lo: 4; z = z_hi * 4 + z_lo), core: 2. Of those that a mesh axis runs over, the one named last changes fastest.
Arguments:
- head_inputs: bfloat16 [131072, 2048], P(('gx', 'gy', 'gz')), may hold values from -6 to 6
- step_raw: float32 [131072, 32], P(('gx', 'gy', 'gz')), may hold values from -4 to 4
- state_in: bfloat16 [131072, 128], P(('gx', 'gy', 'gz')), may hold values from -0.119628906 to 0.119628906
- state_out: bfloat16 [131072, 128], P(('gx', 'gy', 'gz')), may hold values from -0.119628906 to 0.119628906
- decay_log: float32 [32], replicated, may hold values from -13.5 to -3
- step_bias: float32 [32], replicated, may hold values from -1 to 0.5
- skip_gain: float32 [32], replicated, may hold values from 0.5 to 1.5
- checkpoints: bfloat16 [512, 32, 64, 128], P(('gx', 'gy'), None, 'gz'), may hold values from -6 to 6
- out_grad: bfloat16 [131072, 2048], P(('gx', 'gy', 'gz')), may hold values from -6 to 6
Outputs:
- input_grad: bfloat16 [131072, 2048], P(('gx', 'gy', 'gz'))
- step_grad: float32 [131072, 32], P(('gx', 'gy', 'gz'))
- state_in_grad: float32 [131072, 128], P(('gx', 'gy', 'gz'))
- state_out_grad: float32 [131072, 128], P(('gx', 'gy', 'gz'))
- decay_log_grad: float32 [32], replicated
- step_bias_grad: float32 [32], replicated
- skip_gain_grad: float32 [32], replicated
All inputs are finite; a program needn't handle non-finite values.
Results may differ from a plain program's by a relative error of at most 0.00065.
Values may be sent and summed in bfloat16 or wider, within the bound.
A program may use at most 128 MiB of HBM per device.

v0:
```python
import jax
import jax.numpy as jnp
from jax import lax
from jax.sharding import Mesh
from jax.sharding import PartitionSpec as P

GZ = ("gz_0", "gz_1")
GX_GY = ("gx_0", "gx_1", "gy")
GX_GY_GZ = ("gx_0", "gx_1", "gy", "gz_0", "gz_1")
highest = lax.Precision.HIGHEST


def neutral_like(array, identity):
    return jax.tree.map(
        lambda a, e: jnp.broadcast_to(jnp.asarray(e, a.dtype), a.shape), array, identity
    )


def carried_in(array, axes, combine, identity):
    before = start = neutral_like(array, identity)
    so_far = array
    for axis in reversed(axes):
        length, index = (lax.axis_size(axis), lax.axis_index(axis))
        pieces = jax.tree.map(lambda part: lax.all_gather(part, axis), so_far)
        inside, so_far = (start, start)
        for k in reversed(range(length)):
            passed = k > index
            so_far = combine(so_far, jax.tree.map(lambda part: part[k], pieces))
            inside = jax.tree.map(lambda new, old: jnp.where(passed, new, old), so_far, inside)
        before = combine(inside, before)
    return before


def by_axis(array, axes):
    for axis in axes:
        array = lax.psum(array, axis)
    return array


def block_forward(inputs, raw, b_mat, scores, read, decay_log, bias, skip, start):
    step = jax.nn.softplus(raw + bias)
    cum = jnp.cumsum(step * -jnp.exp(decay_log), axis=0)
    length = inputs.shape[0]
    rows = lax.broadcasted_iota(jnp.int32, (length, length), 0)
    cols = lax.broadcasted_iota(jnp.int32, (length, length), 1)
    lower = rows >= cols
    ctrans = cum.T
    gap = ctrans[:, :, None] - ctrans[:, None, :]
    mix = jnp.where(lower, jnp.exp(jnp.where(lower, gap, 0.0)), 0.0) * scores * step.T[:, None, :]
    inner = jnp.einsum("hts,shp->thp", mix, inputs, precision=highest)
    carried = read * jnp.exp(cum)[:, :, None]
    result = inner + carried + skip[None, :, None] * inputs
    tail = jnp.exp(cum[-1][None, :] - cum) * step
    final = jnp.exp(cum[-1])[:, None, None] * start + jnp.einsum(
        "sh,shp,sn->hpn", tail, inputs, b_mat, precision=highest
    )
    return (result, final)


def span_forward(inputs, raw, b_mat, scores, read, decay_log, bias, skip, start):
    length, heads = raw.shape
    width = inputs.shape[1] // heads
    states = start.shape[2]
    block = min(8, heads)
    blocks = heads // block
    grouped = inputs.reshape(length, blocks, block, width).transpose(1, 0, 2, 3)
    read_g = read.reshape(length, blocks, block, width).transpose(1, 0, 2, 3)
    raw_g = raw.reshape(length, blocks, block).transpose(1, 0, 2)

    def one_block(items):
        return block_forward(
            items[0], items[1], b_mat, scores, items[2], items[3], items[4], items[5], items[6]
        )

    result, final = lax.map(
        one_block,
        (
            grouped,
            raw_g,
            read_g,
            decay_log.reshape(blocks, block),
            bias.reshape(blocks, block),
            skip.reshape(blocks, block),
            start.reshape(blocks, block, width, states),
        ),
    )
    result = result.transpose(1, 0, 2, 3).reshape(length, heads * width)
    return (result, final.reshape(heads, width, states))


def combine(earlier, later):
    return (earlier[0] * later[0], later[0][:, None, None] * earlier[1] + later[1])


def local(
    head_inputs,
    step_raw,
    state_in,
    state_out,
    decay_log,
    step_bias,
    skip_gain,
    checkpoints,
    out_grad,
):
    entering = lax.all_to_all(checkpoints, GZ, split_axis=0, concat_axis=2, tiled=True)[0]
    start = entering.astype(jnp.float32)
    length, heads = step_raw.shape
    width = head_inputs.shape[1] // heads
    states = state_in.shape[1]
    c_mat = state_out.astype(jnp.float32)
    b_mat = state_in.astype(jnp.float32)
    grad_rows = out_grad.astype(jnp.float32)
    step = jax.nn.softplus(step_raw + step_bias)
    cum = jnp.cumsum(step * -jnp.exp(decay_log), axis=0)
    weighted = (grad_rows.reshape(length, heads, width) * jnp.exp(cum)[:, :, None]).reshape(
        length, heads * width
    )
    local_term = jnp.dot(weighted.T, c_mat, precision=highest).reshape(heads, width, states)
    decays = jnp.exp(cum[-1])
    group = lax.axis_size(GZ)
    spread = jnp.broadcast_to(decays[None, :, None], (1, heads, group))
    got_decay, got_term = (
        lax.all_to_all(spread, GZ, split_axis=2, concat_axis=0, tiled=True),
        lax.all_to_all(local_term[None], GZ, split_axis=2, concat_axis=0, tiled=True),
    )
    got_decay = got_decay[:, :, 0]
    slice_width = got_term.shape[2]
    suffix_b = jnp.zeros((heads, slice_width, states), jnp.float32)
    suffix_a = jnp.ones((heads,), jnp.float32)
    inners = [None] * group
    leads = [None] * group
    for member in reversed(range(group)):
        inners[member] = suffix_b
        leads[member] = suffix_a
        suffix_b = got_term[member] + got_decay[member][:, None, None] * suffix_b
        suffix_a = got_decay[member] * suffix_a
    total = (suffix_a, suffix_b)
    neutral = (
        jnp.ones((heads,), jnp.float32),
        jnp.zeros((heads, slice_width, states), jnp.float32),
    )
    outer = carried_in(total, GX_GY, combine, neutral)
    carries = jnp.stack(
        [inners[member] + leads[member][:, None, None] * outer[1] for member in range(group)]
    )
    later = lax.all_to_all(carries, GZ, split_axis=0, concat_axis=2, tiled=True)[0]
    flat_start = entering.reshape(heads * width, states)
    scores = jnp.dot(state_out, state_in.T, preferred_element_type=jnp.float32)
    read = jnp.dot(state_out, flat_start.T, preferred_element_type=jnp.float32)
    _, pull = jax.vjp(
        span_forward,
        head_inputs.astype(jnp.float32),
        step_raw,
        b_mat,
        scores,
        read,
        decay_log,
        step_bias,
        skip_gain,
        start,
    )
    grads = pull((grad_rows, later))
    b_grad = grads[2] + jnp.dot(grads[3].T, c_mat, precision=highest)
    c_grad = jnp.dot(grads[3], b_mat, precision=highest) + jnp.dot(
        grads[4], flat_start.astype(jnp.float32), precision=highest
    )
    decay_sum, bias_sum, skip_sum = (
        by_axis(grads[5], GX_GY_GZ),
        by_axis(grads[6], GX_GY_GZ),
        by_axis(grads[7], GX_GY_GZ),
    )
    return (grads[0].astype(jnp.bfloat16), grads[1], b_grad, c_grad, decay_sum, bias_sum, skip_sum)


def solution(mesh):
    torus = Mesh(
        mesh.devices.reshape(4, 2, mesh.shape["gy"], 4, 2), ("gx_0", "gx_1", "gy", "gz_0", "gz_1")
    )
    return jax.shard_map(
        local,
        mesh=torus,
        in_specs=(
            P(GX_GY_GZ, None),
            P(GX_GY_GZ, None),
            P(GX_GY_GZ, None),
            P(GX_GY_GZ, None),
            P(),
            P(),
            P(),
            P(GX_GY, None, GZ, None),
            P(GX_GY_GZ, None),
        ),
        out_specs=(
            P(GX_GY_GZ, None),
            P(GX_GY_GZ, None),
            P(GX_GY_GZ, None),
            P(GX_GY_GZ, None),
            P(),
            P(),
            P(),
        ),
        check_vma=False,
    )
```

profile of v0, /device:TPU:64, one launch (start us, length us, event | category | flops | bytes accessed | tf_op | source)
XLA Modules:
  0.0 441.4 jit_solution(9832343445623595339)
XLA Ops:
  10.4 11.8 %all-to-all-start.1 = ((f32[1,32,8]{1,0,2:T(1,128)}), f32[1,32,8]{1,0,2:T(1,128)S(1)}, u32[]{:S(2)}, u32[]{:S(2)}) async-start(f32[1,32,8]{1,0,2:T(1,128)} %broadcast_in_dim.210), calls=%async_computation.1 | async-start | bytes 8192 | tf_op jit(solution)/shard_map/all_to_all | solution.py:124
  26.7 5.6 %all-to-all-done.1 = f32[1,32,8]{1,0,2:T(1,128)S(1)} async-done(((f32[1,32,8]{1,0,2:T(1,128)}), f32[1,32,8]{1,0,2:T(1,128)S(1)}, u32[]{:S(2)}, u32[]{:S(2)}) %all-to-all-start.1) | async-done | bytes 1056 | tf_op jit(solution)/shard_map/all_to_all | solution.py:124
  32.3 4.0 all-to-all-start
  37.5 29.1 %all-to-all-done = f32[1,32,64,128]{3,1,0,2:T(8,128)S(1)} async-done(((f32[1,32,64,128]{3,1,0,2:T(8,128)}), f32[1,32,64,128]{3,1,0,2:T(8,128)S(1)}, u32[]{:S(2)}, u32[]{:S(2)}) %all-to-all-start) | async-done | bytes 1048608 | tf_op jit(solution)/shard_map/all_to_all | solution.py:125
  68.3 4.2 all-to-all-start.3
  76.8 16.8 %all-gather = f32[8,1,32,1]{2,3,1,0:T(1,128)S(1)} all-gather(f32[1,1,32,1]{2,3,1,0:T(1,128)S(1)} %get-tuple-element.1868), channel_id=2, replica_groups=mesh['gx_0'=4,'gx_1'=2,'gy'=8,'gz_0'=4,'gz_1'=2] {'gy'}, dimensions={0}, use_global_device_ids=true | all-gather | bytes 1152 | tf_op jit(solution)/shard_map/all_gather | solution.py:24
  95.4 8.2 %all-gather.2 = f32[4,1,32]{2,1,0:T(1,128)S(1)} all-gather(f32[1,1,32]{2,1,0:T(1,128)S(1)} %get-tuple-element.1888), channel_id=1, replica_groups=mesh['gx_0'=4,'gx_1'=2,'gy'=8,'gz_0'=4,'gz_1'=2] {'gx_0'}, dimensions={0}, use_global_device_ids=true | all-gather | bytes 640 | tf_op jit(solution)/shard_map/all_gather | solution.py:24
  110.0 16.5 %all_gather.29 = f32[4,32,8,128]{3,2,1,0:T(8,128)S(1)} all-gather(f32[1,32,8,128]{3,2,1,0:T(8,128)S(1)} %slice_add_fusion.4), channel_id=1, replica_groups=mesh['gx_0'=4,'gx_1'=2,'gy'=8,'gz_0'=4,'gz_1'=2] {'gx_0'}, dimensions={0}, use_global_device_ids=true | all-gather | bytes 655360 | tf_op jit(solution)/shard_map/all_gather | solution.py:24
  134.1 6.5 %all-to-all-start.2 = ((f32[8,32,8,128]{3,2,1,0:T(8,128)}), f32[8,32,8,128]{3,2,1,0:T(8,128)}, u32[]{:S(2)}, u32[]{:S(2)}) async-start(f32[8,32,8,128]{3,2,1,0:T(8,128)} %constant_dynamic-update-slice_fusion.3), calls=%async_computation.2 | async-start | bytes 2097152 | tf_op jit(solution)/shard_map/all_to_all | solution.py:147
  145.8 57.4 %while.75 = (s32[]{:T(128)}, f32[4,256,8]{1,2,0:T(8,128)}, f32[4,8]{1,0:T(4,128)}, f32[4,1,8]{2,1,0:T(1,128)}, f32[4,256,8]{1,2,0:T(8,128)}, /*index=5*/f32[4,8,...) while((s32[]{:T(128)}, f32[4,256,8]{1,2,0:T(8,128)}, ...), condition=%wide.region_5.6_spmd.clone.clone, body=%wide.region_2.5_spmd.clone.clone.sunk | while | flops 3090474 | bytes 14180141 | solution.py:75
  147.4 4.2 multiply_dynamic-update-slice_fusion.4
  161.8 4.0 multiply_dynamic-update-slice_fusion.4
  176.1 4.2 multiply_dynamic-update-slice_fusion.4
  190.5 4.0 multiply_dynamic-update-slice_fusion.4
  216.8 157.2 %while.76 = (s32[]{:T(128)}, f32[256,256]{1,0:T(8,128)S(1)}, f32[256,128]{1,0:T(8,128)}, bf16[4,256,8,64]{1,3,2,0:T(8,128)(2,1)}, f32[4,256,8]{1,2,0:T(8,128)}, ...) while((s32[]{:T(128)}, f32[256,256]{1,0:T(8,128)S(1)}, ...), condition=%wide.region_19.20_spmd.clone.clone, body=%wide.region_6.19_spmd.clone.clone.sunk | while | flops 1215725568 | bytes 18326480 | solution.py:75
  222.0 6.5 %fusion.150 = (f32[8,256]{1,0:T(8,128)}, f32[8,256]{1,0:T(8,128)}, f32[256,256]{1,0:T(8,128)S(1)}, f32[8,256]{1,0:T(8,128)}) fusion(f32[4,8,256,256]{3,2,1,0:T(8,128)} %get-tuple-element.2474, s32[]{:T(128)S(6)} %sub.146, f32[256,256]{1,0:T(8,128)S(1)} %bitcast.579, f32[8,256]{1,0:T(8,128)S(1)} %dynamic-slice_bitcast_fusion.6, ...), kind=kOutput, calls=%fused_computation.87.clone.1 | convolution fusion | flops 408348672 | bytes 7964160 | tf_op jit(solution)/shard_map/transpose(jvp())/while/body/eval_jaxpr/hts,shp->thp/dot_general | solution.py:50
  246.7 3.7 fusion.154
  261.3 6.5 %fusion.150 = (f32[8,256]{1,0:T(8,128)}, f32[8,256]{1,0:T(8,128)}, f32[256,256]{1,0:T(8,128)S(1)}, f32[8,256]{1,0:T(8,128)}) fusion(f32[4,8,256,256]{3,2,1,0:T(8,128)} %get-tuple-element.2474, s32[]{:T(128)S(6)} %sub.146, f32[256,256]{1,0:T(8,128)S(1)} %bitcast.579, f32[8,256]{1,0:T(8,128)S(1)} %dynamic-slice_bitcast_fusion.6, ...), kind=kOutput, calls=%fused_computation.87.clone.1 | convolution fusion | flops 408348672 | bytes 7964160 | tf_op jit(solution)/shard_map/transpose(jvp())/while/body/eval_jaxpr/hts,shp->thp/dot_general | solution.py:50
  300.6 6.5 %fusion.150 = (f32[8,256]{1,0:T(8,128)}, f32[8,256]{1,0:T(8,128)}, f32[256,256]{1,0:T(8,128)S(1)}, f32[8,256]{1,0:T(8,128)}) fusion(f32[4,8,256,256]{3,2,1,0:T(8,128)} %get-tuple-element.2474, s32[]{:T(128)S(6)} %sub.146, f32[256,256]{1,0:T(8,128)S(1)} %bitcast.579, f32[8,256]{1,0:T(8,128)S(1)} %dynamic-slice_bitcast_fusion.6, ...), kind=kOutput, calls=%fused_computation.87.clone.1 | convolution fusion | flops 408348672 | bytes 7964160 | tf_op jit(solution)/shard_map/transpose(jvp())/while/body/eval_jaxpr/hts,shp->thp/dot_general | solution.py:50
  339.9 6.5 %fusion.150 = (f32[8,256]{1,0:T(8,128)}, f32[8,256]{1,0:T(8,128)}, f32[256,256]{1,0:T(8,128)S(1)}, f32[8,256]{1,0:T(8,128)}) fusion(f32[4,8,256,256]{3,2,1,0:T(8,128)} %get-tuple-element.2474, s32[]{:T(128)S(6)} %sub.146, f32[256,256]{1,0:T(8,128)S(1)} %bitcast.579, f32[8,256]{1,0:T(8,128)S(1)} %dynamic-slice_bitcast_fusion.6, ...), kind=kOutput, calls=%fused_computation.87.clone.1 | convolution fusion | flops 408348672 | bytes 7964160 | tf_op jit(solution)/shard_map/transpose(jvp())/while/body/eval_jaxpr/hts,shp->thp/dot_general | solution.py:50
  381.7 11.6 %all-reduce.4 = (f32[32]{0:T(128)S(1)}, f32[32]{0:T(128)S(1)}, f32[32]{0:T(128)S(1)}) all-reduce(f32[32]{0:T(128)S(1)} %reshape.895, f32[32]{0:T(128)S(1)} %reshape.896, f32[32]{0:T(128)S(1)} %reshape.897), channel_id=1, replica_groups=mesh['gx_0'=4,'gx_1'=2,'gy'=8,'gz_0'=4,'gz_1'=2] {'gx_0'}, use_global_device_ids=true, to_apply=%region_20.21 | all-reduce | flops 96 | bytes 768 | tf_op jit(solution)/shard_map/psum | solution.py:36
  395.8 16.1 %all-reduce.2 = (f32[32]{0:T(128)S(1)}, f32[32]{0:T(128)S(1)}, f32[32]{0:T(128)S(1)}) all-reduce(f32[32]{0:T(128)S(1)} %get-tuple-element.1825, f32[32]{0:T(128)S(1)} %get-tuple-element.1826, f32[32]{0:T(128)S(1)} %get-tuple-element.1827), channel_id=1, replica_groups=mesh['gx_0'=4,'gx_1'=2,'gy'=8,'gz_0'=4,'gz_1'=2] {'gy'}, use_global_device_ids=true, to_apply=%region_22.23 | all-reduce | flops 96 | bytes 768 | tf_op jit(solution)/shard_map/psum | solution.py:36
  411.8 10.9 %all-reduce.3 = (f32[32]{0:T(128)S(1)}, f32[32]{0:T(128)S(1)}, f32[32]{0:T(128)S(1)}) all-reduce(f32[32]{0:T(128)S(1)} %get-tuple-element.1813, f32[32]{0:T(128)S(1)} %get-tuple-element.1814, f32[32]{0:T(128)S(1)} %get-tuple-element.1815), channel_id=1, replica_groups=mesh['gx_0'=4,'gx_1'=2,'gy'=8,'gz_0'=4,'gz_1'=2] {'gz_0'}, use_global_device_ids=true, to_apply=%region_23.24 | all-reduce | flops 96 | bytes 768 | tf_op jit(solution)/shard_map/psum | solution.py:36
  422.8 9.3 %all-reduce.5 = (f32[32]{0:T(128)}, f32[32]{0:T(128)}, f32[32]{0:T(128)}) all-reduce(f32[32]{0:T(128)S(1)} %get-tuple-element.1816, f32[32]{0:T(128)S(1)} %get-tuple-element.1817, f32[32]{0:T(128)S(1)} %get-tuple-element.1818), channel_id=1, replica_groups=mesh['gx_0'=4,'gx_1'=2,'gy'=8,'gz_0'=4,'gz_1'=2] {'gz_1'}, use_global_device_ids=true, to_apply=%region_24.25 | all-reduce | flops 96 | bytes 768 | tf_op jit(solution)/shard_map/psum | solution.py:36
  (380 shorter events, 229.9 us)
Async XLA Ops:
  10.4 21.9 %all-to-all-start.1 = ((f32[1,32,8]{1,0,2:T(1,128)}), f32[1,32,8]{1,0,2:T(1,128)S(1)}, u32[]{:S(2)}, u32[]{:S(2)}) async-start(f32[1,32,8]{1,0,2:T(1,128)} %broadcast_in_dim.210), calls=%async_computation.1 | async-start | bytes 8192 | tf_op jit(solution)/shard_map/all_to_all | solution.py:124
  32.3 34.3 %all-to-all-start = ((f32[1,32,64,128]{3,1,0,2:T(8,128)}), f32[1,32,64,128]{3,1,0,2:T(8,128)S(1)}, u32[]{:S(2)}, u32[]{:S(2)}) async-start(f32[1,32,64,128]{3,1,0,2:T(8,128)} %copy.171), calls=%async_computation | async-start | bytes 2097152 | tf_op jit(solution)/shard_map/all_to_all | solution.py:125
  36.3 69.5 %all-gather.5.cloned.1.call-start = ((), (), s32[]{:S(2)}) async-start(), calls=%async_computation.4 | async-start | bytes 1179648 | tf_op jit(solution)/shard_map/all_gather | solution.py:24
  37.0 31.3 %copy-start.18 = (f32[32]{0:T(128)}, f32[32]{0:T(128)S(1)}, u32[]{:S(2)}) copy-start(f32[32]{0:T(128)S(1)} %get-tuple-element.1883) | copy-start | bytes 388
  37.4 30.9 %copy-start.20 = (f32[32]{0:T(128)}, f32[32]{0:T(128)S(1)}, u32[]{:S(2)}) copy-start(f32[32]{0:T(128)S(1)} %get-tuple-element.1874) | copy-start | bytes 388
  37.4 30.9 %copy-start.22 = (f32[32]{0:T(128)}, f32[32]{0:T(128)S(1)}, u32[]{:S(2)}) copy-start(f32[32]{0:T(128)S(1)} %get-tuple-element.1870) | copy-start | bytes 388
  37.4 30.9 %copy-start.24 = (f32[32]{0:T(128)}, f32[32]{0:T(128)S(1)}, u32[]{:S(2)}) copy-start(f32[32]{0:T(128)S(1)} %get-tuple-element.1872) | copy-start | bytes 388
  37.4 35.2 %copy-start.31 = (f32[32]{0:T(128)S(1)}, f32[32]{0:T(128)}, u32[]{:S(2)}) copy-start(f32[32]{0:T(128)} %param.18) | copy-start | bytes 388
  37.5 35.8 %copy-start.41 = (f32[32]{0:T(128)S(1)}, f32[32]{0:T(128)}, u32[]{:S(2)}) copy-start(f32[32]{0:T(128)} %param.17) | copy-start | bytes 388
  68.3 65.7 %all-to-all-start.3 = ((bf16[8,32,8,128]{3,2,1,0:T(8,128)(2,1)}), bf16[8,32,8,128]{3,2,1,0:T(8,128)(2,1)}, u32[]{:S(2)}, u32[]{:S(2)}) async-start(bf16[8,32,8,128]{3,2,1,0:T(8,128)(2,1)} %param.20), calls=%async_computation.3 | async-start | bytes 1048576 | tf_op jit(solution)/shard_map/all_to_all | solution.py:106
  105.8 20.7 %copy-start.35 = (f32[32]{0:T(128)S(1)}, f32[32]{0:T(128)}, u32[]{:S(2)}) copy-start(f32[32]{0:T(128)} %get-tuple-element.1884) | copy-start | bytes 388
  105.8 20.7 %copy-start.36 = (f32[32]{0:T(128)S(1)}, f32[32]{0:T(128)}, u32[]{:S(2)}) copy-start(f32[32]{0:T(128)} %get-tuple-element.1885) | copy-start | bytes 388
  105.8 20.7 %copy-start.37 = (f32[32]{0:T(128)S(1)}, f32[32]{0:T(128)}, u32[]{:S(2)}) copy-start(f32[32]{0:T(128)} %get-tuple-element.1886) | copy-start | bytes 388
  105.9 20.7 %copy-start.38 = (f32[32]{0:T(128)S(1)}, f32[32]{0:T(128)}, u32[]{:S(2)}) copy-start(f32[32]{0:T(128)} %get-tuple-element.1887) | copy-start | bytes 388
  107.6 21.2 %copy-start.30 = (f32[32]{0:T(128)S(1)}, f32[32]{0:T(128)}, u32[]{:S(2)}) copy-start(f32[32]{0:T(128)} %get-tuple-element.1839) | copy-start | bytes 388
  107.6 21.9 %copy-start.7 = (f32[1,32,8,128]{3,2,1,0:T(8,128)S(1)}, f32[1,32,8,128]{3,2,1,0:T(8,128)}, u32[]{:S(2)}) copy-start(f32[1,32,8,128]{3,2,1,0:T(8,128)} %get-tuple-element.1850) | copy-start | bytes 393220
  107.6 21.9 %copy-start.25 = (f32[32]{0:T(128)S(1)}, f32[32]{0:T(128)}, u32[]{:S(2)}) copy-start(f32[32]{0:T(128)} %copy-done.24) | copy-start | bytes 388
  107.7 21.9 %copy-start.40 = (f32[32]{0:T(128)S(1)}, f32[32]{0:T(128)}, u32[]{:S(2)}) copy-start(f32[32]{0:T(128)} %get-tuple-element.1840) | copy-start | bytes 388
  109.9 21.2 %copy-start.6 = (f32[1,32,8,128]{3,2,1,0:T(8,128)S(1)}, f32[1,32,8,128]{3,2,1,0:T(8,128)}, u32[]{:S(2)}) copy-start(f32[1,32,8,128]{3,2,1,0:T(8,128)} %get-tuple-element.1851) | copy-start | bytes 393220
  109.9 21.1 %copy-start.23 = (f32[32]{0:T(128)S(1)}, f32[32]{0:T(128)}, u32[]{:S(2)}) copy-start(f32[32]{0:T(128)} %copy-done.22) | copy-start | bytes 388
  110.0 21.1 %copy-start.39 = (f32[32]{0:T(128)S(1)}, f32[32]{0:T(128)}, u32[]{:S(2)}) copy-start(f32[32]{0:T(128)} %get-tuple-element.1842) | copy-start | bytes 388
  134.1 76.5 %all-to-all-start.2 = ((f32[8,32,8,128]{3,2,1,0:T(8,128)}), f32[8,32,8,128]{3,2,1,0:T(8,128)}, u32[]{:S(2)}, u32[]{:S(2)}) async-start(f32[8,32,8,128]{3,2,1,0:T(8,128)} %constant_dynamic-update-slice_fusion.3), calls=%async_computation.2 | async-start | bytes 2097152 | tf_op jit(solution)/shard_map/all_to_all | solution.py:147
  374.0 58.1 %copy-start.2 = (f32[4,256,8,64]{1,3,2,0:T(8,128)S(1)}, f32[4,256,8,64]{1,3,2,0:T(8,128)}, u32[]{:S(2)}) copy-start(f32[4,256,8,64]{1,3,2,0:T(8,128)} %get-tuple-element.1033) | copy-start | bytes 6291460
  374.0 58.1 %copy-start.4 = (bf16[8,32,8,128]{3,2,0,1:T(8,128)(2,1)S(1)}, bf16[8,32,8,128]{3,2,0,1:T(8,128)(2,1)}, u32[]{:S(2)}) copy-start(bf16[8,32,8,128]{3,2,0,1:T(8,128)(2,1)} %copy-done.3) | copy-start | bytes 1572868
  (33 other events, 270.8 us)
Sparse Core Ops, SparseCore 0:
  68.4 37.3 all-gather.4
where the time goes:
time: 445 us; the launch traced here: 441 us
  local copies, waits for them, and re-layouts  99.1 us (22%)
  other arithmetic  98.9 us (22%)
  blocking collectives  95.8 us (22%)
  matrix products  70.4 us (16%)
  waiting for transfers between devices  35.7 us (8%)
  starting transfers between devices  26.6 us (6%)
  between operations  14.6 us (3%)
    psum x5, blocking collectives, by_axis(): array = lax.psum(array, axis)  50.4 us
    all_gather x5, blocking collectives, carried_in(): pieces = jax.tree.map(lambda part: lax.all_gather(part, axis), so_far)  45.4 us
    dot_general x8, matrix products, block_forward(): inner = jnp.einsum('hts,shp->thp', mix, inputs, precision=highest)  40.7 us
    dynamic_update_slice x36, local copies, waits for them, and re-layouts, span_forward(): lax.map(one_block, (grouped, raw_g, read_g, decay_log.reshape(blocks, blo...  32.7 us
    dynamic_update_slice x24, other arithmetic, span_forward(): lax.map(one_block, (grouped, raw_g, read_g, decay_log.reshape(blocks, blo...  30.3 us
    all_to_all x1, waiting for transfers between devices, local(): lax.all_to_all(local_term[None], GZ, split_axis=2, concat_axis=0, tiled=T...  29.1 us
    another operation x33, other arithmetic  27.8 us
    dot_general x8, matrix products, block_forward(): jnp.einsum('sh,shp,sn->hpn', tail, inputs, b_mat, precision=highest)  21.1 us
  transfers between devices with their start and end apart: 5, of which 3 were waited for; matrix products, arithmetic and copies ran while one was open for 20% of the time, Pallas kernels for 0%

commit v1 on v0

--- a/solution.py
+++ b/solution.py
@@ -33,7 +33,10 @@
 
 def by_axis(array, axes):
     for axis in axes:
-        array = lax.psum(array, axis)
+        store_columns_here = lambda x_local, across: jnp.sum(
+            jax.lax.all_gather(x_local, across), axis=0
+        )
+        array = store_columns_here(array, axis)
     return array
 
 

time: 445 us -> 475 us (1.067)
  blocking collectives: 95.8 us -> 112 us
  local copies, waits for them, and re-layouts: 99.1 us -> 108 us
    psum x5 -> x0, blocking collectives: 50.4 us -> none  [by_axis(): array = lax.psum(array, axis)]
    unnamed x0 -> x4, blocking collectives: none -> 38.2 us
    all_gather x0 -> x3, blocking collectives: none -> 28.2 us  [by_axis(): jax.lax.all_gather(x_local, across)]
    unnamed x82 -> x113, local copies, waits for them, and re-layouts: 3.92 us -> 14.1 us
where the time goes in v1:
time: 475 us; the launch traced here: 471 us
  blocking collectives  112 us (24%)
  local copies, waits for them, and re-layouts  108 us (23%)
  other arithmetic  101 us (21%)
  matrix products  70.6 us (15%)
  waiting for transfers between devices  35.7 us (8%)
  starting transfers between devices  26.6 us (6%)
  between operations  17.3 us (4%)
    all_gather x5, blocking collectives, carried_in(): pieces = jax.tree.map(lambda part: lax.all_gather(part, axis), so_far)  45.4 us
    dot_general x8, matrix products, block_forward(): inner = jnp.einsum('hts,shp->thp', mix, inputs, precision=highest)  40.6 us
    unnamed x4, blocking collectives  38.2 us
    dynamic_update_slice x36, local copies, waits for them, and re-layouts, span_forward(): lax.map(one_block, (grouped, raw_g, read_g, decay_log.reshape(blocks, blo...  32.7 us
    dynamic_update_slice x24, other arithmetic, span_forward(): lax.map(one_block, (grouped, raw_g, read_g, decay_log.reshape(blocks, blo...  30.3 us
    all_to_all x1, waiting for transfers between devices, local(): lax.all_to_all(local_term[None], GZ, split_axis=2, concat_axis=0, tiled=T...  29.1 us
    all_gather x3, blocking collectives, by_axis(): jax.lax.all_gather(x_local, across)  28.2 us
    another operation x33, other arithmetic  27.8 us
  transfers between devices with their start and end apart: 5, of which 3 were waited for; matrix products, arithmetic and copies ran while one was open for 20% of the time, Pallas kernels for 0%

profile of v1, /device:TPU:64, one launch (start us, length us, event | category | flops | bytes accessed | tf_op | source)
XLA Modules:
  0.0 471.2 jit_solution(2877582283976164522)
XLA Ops:
  10.4 11.8 %all-to-all-start.1 = ((f32[1,32,8]{1,0,2:T(1,128)}), f32[1,32,8]{1,0,2:T(1,128)S(1)}, u32[]{:S(2)}, u32[]{:S(2)}) async-start(f32[1,32,8]{1,0,2:T(1,128)} %broadcast_in_dim.210), calls=%async_computation.1 | async-start | bytes 8192 | tf_op jit(solution)/shard_map/all_to_all | solution.py:127
  26.7 5.6 %all-to-all-done.1 = f32[1,32,8]{1,0,2:T(1,128)S(1)} async-done(((f32[1,32,8]{1,0,2:T(1,128)}), f32[1,32,8]{1,0,2:T(1,128)S(1)}, u32[]{:S(2)}, u32[]{:S(2)}) %all-to-all-start.1) | async-done | bytes 1056 | tf_op jit(solution)/shard_map/all_to_all | solution.py:127
  32.3 4.0 all-to-all-start
  37.5 29.1 %all-to-all-done = f32[1,32,64,128]{3,1,0,2:T(8,128)S(1)} async-done(((f32[1,32,64,128]{3,1,0,2:T(8,128)}), f32[1,32,64,128]{3,1,0,2:T(8,128)S(1)}, u32[]{:S(2)}, u32[]{:S(2)}) %all-to-all-start) | async-done | bytes 1048608 | tf_op jit(solution)/shard_map/all_to_all | solution.py:128
  68.3 4.2 all-to-all-start.3
  76.8 16.8 %all-gather = f32[8,1,32,1]{2,3,1,0:T(1,128)S(1)} all-gather(f32[1,1,32,1]{2,3,1,0:T(1,128)S(1)} %get-tuple-element.1929), channel_id=2, replica_groups=mesh['gx_0'=4,'gx_1'=2,'gy'=8,'gz_0'=4,'gz_1'=2] {'gy'}, dimensions={0}, use_global_device_ids=true | all-gather | bytes 1152 | tf_op jit(solution)/shard_map/all_gather | solution.py:24
  95.4 8.2 %all-gather.14 = f32[4,1,32]{2,1,0:T(1,128)S(1)} all-gather(f32[1,1,32]{2,1,0:T(1,128)S(1)} %get-tuple-element.1949), channel_id=1, replica_groups=mesh['gx_0'=4,'gx_1'=2,'gy'=8,'gz_0'=4,'gz_1'=2] {'gx_0'}, dimensions={0}, use_global_device_ids=true | all-gather | bytes 640 | tf_op jit(solution)/shard_map/all_gather | solution.py:24
  110.0 16.5 %all_gather.110 = f32[4,32,8,128]{3,2,1,0:T(8,128)S(1)} all-gather(f32[1,32,8,128]{3,2,1,0:T(8,128)S(1)} %slice_add_fusion.4), channel_id=1, replica_groups=mesh['gx_0'=4,'gx_1'=2,'gy'=8,'gz_0'=4,'gz_1'=2] {'gx_0'}, dimensions={0}, use_global_device_ids=true | all-gather | bytes 655360 | tf_op jit(solution)/shard_map/all_gather | solution.py:24
  134.1 6.5 %all-to-all-start.2 = ((f32[8,32,8,128]{3,2,1,0:T(8,128)}), f32[8,32,8,128]{3,2,1,0:T(8,128)}, u32[]{:S(2)}, u32[]{:S(2)}) async-start(f32[8,32,8,128]{3,2,1,0:T(8,128)} %constant_dynamic-update-slice_fusion.3), calls=%async_computation.2 | async-start | bytes 2097152 | tf_op jit(solution)/shard_map/all_to_all | solution.py:150
  145.8 57.4 %while.75 = (s32[]{:T(128)}, f32[4,256,8]{1,2,0:T(8,128)}, f32[4,8]{1,0:T(4,128)}, f32[4,1,8]{2,1,0:T(1,128)}, f32[4,256,8]{1,2,0:T(8,128)}, /*index=5*/f32[4,8,...) while((s32[]{:T(128)}, f32[4,256,8]{1,2,0:T(8,128)}, ...), condition=%wide.region_5.6_spmd.clone.clone, body=%wide.region_2.5_spmd.clone.clone.sunk | while | flops 3090474 | bytes 14180141 | solution.py:78
  147.4 4.2 multiply_dynamic-update-slice_fusion.4
  176.1 4.2 multiply_dynamic-update-slice_fusion.4
  190.5 4.0 multiply_dynamic-update-slice_fusion.4
  224.4 157.7 %while.76 = (s32[]{:T(128)}, f32[256,256]{1,0:T(8,128)S(1)}, f32[256,128]{1,0:T(8,128)}, bf16[4,256,8,64]{1,3,2,0:T(8,128)(2,1)}, f32[4,256,8]{1,2,0:T(8,128)}, ...) while((s32[]{:T(128)}, f32[256,256]{1,0:T(8,128)S(1)}, ...), condition=%wide.region_19.20_spmd.clone.clone, body=%wide.region_6.19_spmd.clone.clone.sunk | while | flops 1215725568 | bytes 18326480 | solution.py:78
  229.8 6.5 %fusion.150 = (f32[8,256]{1,0:T(8,128)}, f32[8,256]{1,0:T(8,128)}, f32[256,256]{1,0:T(8,128)S(1)}, f32[8,256]{1,0:T(8,128)}) fusion(f32[4,8,256,256]{3,2,1,0:T(8,128)} %get-tuple-element.2535, s32[]{:T(128)S(6)} %sub.146, f32[256,256]{1,0:T(8,128)S(1)} %bitcast.583, f32[8,256]{1,0:T(8,128)S(1)} %dynamic-slice_bitcast_fusion.6, ...), kind=kOutput, calls=%fused_computation.87.clone.1 | convolution fusion | flops 408348672 | bytes 7964160 | tf_op jit(solution)/shard_map/transpose(jvp())/while/body/eval_jaxpr/hts,shp->thp/dot_general | solution.py:53
  269.2 6.5 %fusion.150 = (f32[8,256]{1,0:T(8,128)}, f32[8,256]{1,0:T(8,128)}, f32[256,256]{1,0:T(8,128)S(1)}, f32[8,256]{1,0:T(8,128)}) fusion(f32[4,8,256,256]{3,2,1,0:T(8,128)} %get-tuple-element.2535, s32[]{:T(128)S(6)} %sub.146, f32[256,256]{1,0:T(8,128)S(1)} %bitcast.583, f32[8,256]{1,0:T(8,128)S(1)} %dynamic-slice_bitcast_fusion.6, ...), kind=kOutput, calls=%fused_computation.87.clone.1 | convolution fusion | flops 408348672 | bytes 7964160 | tf_op jit(solution)/shard_map/transpose(jvp())/while/body/eval_jaxpr/hts,shp->thp/dot_general | solution.py:53
  308.6 6.5 %fusion.150 = (f32[8,256]{1,0:T(8,128)}, f32[8,256]{1,0:T(8,128)}, f32[256,256]{1,0:T(8,128)S(1)}, f32[8,256]{1,0:T(8,128)}) fusion(f32[4,8,256,256]{3,2,1,0:T(8,128)} %get-tuple-element.2535, s32[]{:T(128)S(6)} %sub.146, f32[256,256]{1,0:T(8,128)S(1)} %bitcast.583, f32[8,256]{1,0:T(8,128)S(1)} %dynamic-slice_bitcast_fusion.6, ...), kind=kOutput, calls=%fused_computation.87.clone.1 | convolution fusion | flops 408348672 | bytes 7964160 | tf_op jit(solution)/shard_map/transpose(jvp())/while/body/eval_jaxpr/hts,shp->thp/dot_general | solution.py:53
  348.0 6.5 %fusion.150 = (f32[8,256]{1,0:T(8,128)}, f32[8,256]{1,0:T(8,128)}, f32[256,256]{1,0:T(8,128)S(1)}, f32[8,256]{1,0:T(8,128)}) fusion(f32[4,8,256,256]{3,2,1,0:T(8,128)} %get-tuple-element.2535, s32[]{:T(128)S(6)} %sub.146, f32[256,256]{1,0:T(8,128)S(1)} %bitcast.583, f32[8,256]{1,0:T(8,128)S(1)} %dynamic-slice_bitcast_fusion.6, ...), kind=kOutput, calls=%fused_computation.87.clone.1 | convolution fusion | flops 408348672 | bytes 7964160 | tf_op jit(solution)/shard_map/transpose(jvp())/while/body/eval_jaxpr/hts,shp->thp/dot_general | solution.py:53
  383.0 10.8 %all-gather.15 = f32[4,1,32]{2,1,0:T(1,128)S(1)} all-gather(f32[1,1,32]{2,1,0:T(1,128)S(1)} %reshape.982), channel_id=1, replica_groups=mesh['gx_0'=4,'gx_1'=2,'gy'=8,'gz_0'=4,'gz_1'=2] {'gx_0'}, dimensions={0}, use_global_device_ids=true | all-gather | bytes 640 | tf_op jit(solution)/shard_map/all_gather | solution.py:37
  394.6 8.3 %all-gather.16 = f32[4,1,32]{2,1,0:T(1,128)S(1)} all-gather(f32[1,1,32]{2,1,0:T(1,128)S(1)} %reshape.984), channel_id=1, replica_groups=mesh['gx_0'=4,'gx_1'=2,'gy'=8,'gz_0'=4,'gz_1'=2] {'gx_0'}, dimensions={0}, use_global_device_ids=true | all-gather | bytes 640 | tf_op jit(solution)/shard_map/all_gather | solution.py:37
  403.6 9.1 %all-gather.17 = f32[4,1,32]{2,1,0:T(1,128)S(1)} all-gather(f32[1,1,32]{2,1,0:T(1,128)S(1)} %reshape.986), channel_id=1, replica_groups=mesh['gx_0'=4,'gx_1'=2,'gy'=8,'gz_0'=4,'gz_1'=2] {'gx_0'}, dimensions={0}, use_global_device_ids=true | all-gather | bytes 640 | tf_op jit(solution)/shard_map/all_gather | solution.py:37
  416.9 16.1 %all-reduce.14 = (f32[256]{0:T(256)S(1)}, f32[256]{0:T(256)S(1)}, f32[256]{0:T(256)S(1)}) all-reduce(f32[256]{0:T(256)S(1)} %dynamic-update-slice.1, f32[256]{0:T(256)S(1)} %dynamic-update-slice.5, f32[256]{0:T(256)S(1)} %dynamic-update-slice.9), channel_id=4, replica_groups=mesh['gx_0'=4,'gx_1'=2,'gy'=8,'gz_0'=4,'gz_1'=2] {'gy'}, use_global_device_ids=true, to_apply=%add.3 | all-reduce | flops 768 | bytes 6144
  433.9 10.9 %all-reduce.15 = (f32[128]{0:T(128)S(1)}, f32[128]{0:T(128)S(1)}, f32[128]{0:T(128)S(1)}) all-reduce(f32[128]{0:T(128)S(1)} %dynamic-update-slice.2, f32[128]{0:T(128)S(1)} %dynamic-update-slice.6, f32[128]{0:T(128)S(1)} %dynamic-update-slice.10), channel_id=5, replica_groups=mesh['gx_0'=4,'gx_1'=2,'gy'=8,'gz_0'=4,'gz_1'=2] {'gz_0'}, use_global_device_ids=true, to_apply=%add.4 | all-reduce | flops 384 | bytes 3072
  445.9 8.8 %all-reduce.16 = (f32[64]{0:T(128)S(1)}, f32[64]{0:T(128)S(1)}, f32[64]{0:T(128)S(1)}) all-reduce(f32[64]{0:T(128)S(1)} %dynamic-update-slice.3, f32[64]{0:T(128)S(1)} %dynamic-update-slice.7, f32[64]{0:T(128)S(1)} %dynamic-update-slice.11), channel_id=6, replica_groups=mesh['gx_0'=4,'gx_1'=2,'gy'=8,'gz_0'=4,'gz_1'=2] {'gz_1'}, use_global_device_ids=true, to_apply=%add.5 | all-reduce | flops 192 | bytes 1536
  (437 shorter events, 248.7 us)
Async XLA Ops:
  10.4 21.9 %all-to-all-start.1 = ((f32[1,32,8]{1,0,2:T(1,128)}), f32[1,32,8]{1,0,2:T(1,128)S(1)}, u32[]{:S(2)}, u32[]{:S(2)}) async-start(f32[1,32,8]{1,0,2:T(1,128)} %broadcast_in_dim.210), calls=%async_computation.1 | async-start | bytes 8192 | tf_op jit(solution)/shard_map/all_to_all | solution.py:127
  32.3 34.3 %all-to-all-start = ((f32[1,32,64,128]{3,1,0,2:T(8,128)}), f32[1,32,64,128]{3,1,0,2:T(8,128)S(1)}, u32[]{:S(2)}, u32[]{:S(2)}) async-start(f32[1,32,64,128]{3,1,0,2:T(8,128)} %copy.195), calls=%async_computation | async-start | bytes 2097152 | tf_op jit(solution)/shard_map/all_to_all | solution.py:128
  36.3 69.5 %all-gather.20.cloned.1.call-start = ((), (), s32[]{:S(2)}) async-start(), calls=%async_computation.4 | async-start | bytes 1179648 | tf_op jit(solution)/shard_map/all_gather | solution.py:24
  37.0 31.3 %copy-start.18 = (f32[32]{0:T(128)}, f32[32]{0:T(128)S(1)}, u32[]{:S(2)}) copy-start(f32[32]{0:T(128)S(1)} %get-tuple-element.1944) | copy-start | bytes 388
  37.4 30.9 %copy-start.20 = (f32[32]{0:T(128)}, f32[32]{0:T(128)S(1)}, u32[]{:S(2)}) copy-start(f32[32]{0:T(128)S(1)} %get-tuple-element.1935) | copy-start | bytes 388
  37.4 30.9 %copy-start.22 = (f32[32]{0:T(128)}, f32[32]{0:T(128)S(1)}, u32[]{:S(2)}) copy-start(f32[32]{0:T(128)S(1)} %get-tuple-element.1931) | copy-start | bytes 388
  37.4 30.9 %copy-start.24 = (f32[32]{0:T(128)}, f32[32]{0:T(128)S(1)}, u32[]{:S(2)}) copy-start(f32[32]{0:T(128)S(1)} %get-tuple-element.1933) | copy-start | bytes 388
  37.4 35.2 %copy-start.31 = (f32[32]{0:T(128)S(1)}, f32[32]{0:T(128)}, u32[]{:S(2)}) copy-start(f32[32]{0:T(128)} %param.18) | copy-start | bytes 388
  37.5 35.8 %copy-start.41 = (f32[32]{0:T(128)S(1)}, f32[32]{0:T(128)}, u32[]{:S(2)}) copy-start(f32[32]{0:T(128)} %param.17) | copy-start | bytes 388
  68.3 65.7 %all-to-all-start.3 = ((bf16[8,32,8,128]{3,2,1,0:T(8,128)(2,1)}), bf16[8,32,8,128]{3,2,1,0:T(8,128)(2,1)}, u32[]{:S(2)}, u32[]{:S(2)}) async-start(bf16[8,32,8,128]{3,2,1,0:T(8,128)(2,1)} %param.20), calls=%async_computation.3 | async-start | bytes 1048576 | tf_op jit(solution)/shard_map/all_to_all | solution.py:109
  105.8 20.7 %copy-start.35 = (f32[32]{0:T(128)S(1)}, f32[32]{0:T(128)}, u32[]{:S(2)}) copy-start(f32[32]{0:T(128)} %get-tuple-element.1945) | copy-start | bytes 388
  105.8 20.7 %copy-start.36 = (f32[32]{0:T(128)S(1)}, f32[32]{0:T(128)}, u32[]{:S(2)}) copy-start(f32[32]{0:T(128)} %get-tuple-element.1946) | copy-start | bytes 388
  105.8 20.7 %copy-start.37 = (f32[32]{0:T(128)S(1)}, f32[32]{0:T(128)}, u32[]{:S(2)}) copy-start(f32[32]{0:T(128)} %get-tuple-element.1947) | copy-start | bytes 388
  105.9 20.7 %copy-start.38 = (f32[32]{0:T(128)S(1)}, f32[32]{0:T(128)}, u32[]{:S(2)}) copy-start(f32[32]{0:T(128)} %get-tuple-element.1948) | copy-start | bytes 388
  107.6 21.2 %copy-start.30 = (f32[32]{0:T(128)S(1)}, f32[32]{0:T(128)}, u32[]{:S(2)}) copy-start(f32[32]{0:T(128)} %get-tuple-element.1900) | copy-start | bytes 388
  107.6 21.9 %copy-start.7 = (f32[1,32,8,128]{3,2,1,0:T(8,128)S(1)}, f32[1,32,8,128]{3,2,1,0:T(8,128)}, u32[]{:S(2)}) copy-start(f32[1,32,8,128]{3,2,1,0:T(8,128)} %get-tuple-element.1911) | copy-start | bytes 393220
  107.6 21.9 %copy-start.25 = (f32[32]{0:T(128)S(1)}, f32[32]{0:T(128)}, u32[]{:S(2)}) copy-start(f32[32]{0:T(128)} %copy-done.24) | copy-start | bytes 388
  107.7 21.9 %copy-start.40 = (f32[32]{0:T(128)S(1)}, f32[32]{0:T(128)}, u32[]{:S(2)}) copy-start(f32[32]{0:T(128)} %get-tuple-element.1901) | copy-start | bytes 388
  109.9 21.2 %copy-start.6 = (f32[1,32,8,128]{3,2,1,0:T(8,128)S(1)}, f32[1,32,8,128]{3,2,1,0:T(8,128)}, u32[]{:S(2)}) copy-start(f32[1,32,8,128]{3,2,1,0:T(8,128)} %get-tuple-element.1912) | copy-start | bytes 393220
  109.9 21.1 %copy-start.23 = (f32[32]{0:T(128)S(1)}, f32[32]{0:T(128)}, u32[]{:S(2)}) copy-start(f32[32]{0:T(128)} %copy-done.22) | copy-start | bytes 388
  110.0 21.1 %copy-start.39 = (f32[32]{0:T(128)S(1)}, f32[32]{0:T(128)}, u32[]{:S(2)}) copy-start(f32[32]{0:T(128)} %get-tuple-element.1903) | copy-start | bytes 388
  134.1 84.2 %all-to-all-start.2 = ((f32[8,32,8,128]{3,2,1,0:T(8,128)}), f32[8,32,8,128]{3,2,1,0:T(8,128)}, u32[]{:S(2)}, u32[]{:S(2)}) async-start(f32[8,32,8,128]{3,2,1,0:T(8,128)} %constant_dynamic-update-slice_fusion.3), calls=%async_computation.2 | async-start | bytes 2097152 | tf_op jit(solution)/shard_map/all_to_all | solution.py:150
  382.1 79.7 %copy-start.2 = (f32[4,256,8,64]{1,3,2,0:T(8,128)S(1)}, f32[4,256,8,64]{1,3,2,0:T(8,128)}, u32[]{:S(2)}) copy-start(f32[4,256,8,64]{1,3,2,0:T(8,128)} %get-tuple-element.1033) | copy-start | bytes 6291460
  382.1 79.7 %copy-start.4 = (bf16[8,32,8,128]{3,2,0,1:T(8,128)(2,1)S(1)}, bf16[8,32,8,128]{3,2,0,1:T(8,128)(2,1)}, u32[]{:S(2)}) copy-start(bf16[8,32,8,128]{3,2,0,1:T(8,128)(2,1)} %copy-done.3) | copy-start | bytes 1572868
  (33 other events, 270.7 us)
Sparse Core Ops, SparseCore 0:
  68.4 37.3 all-gather.19
